TPU v7x, 256 devices: a whole 4x4x8 slice. The times are simulated.
256 devices in a mesh: client: 16 (over y_lo, z), tensor: 8 (over x, core), sdata: 2 (over y_hi).
Axes of the slice: x: 4, y: 4 (y_hi: 2, y_lo: 2; y = y_hi * 2 + y_lo), z: 8, core: 2. Of those that a mesh axis runs over, the one named last changes fastest.
Arguments:
- client_input: bfloat16 [12288, 2048], P(('client', 'sdata')), may hold values from -6 to 6
- client_gain: bfloat16 [16, 2048], P('client'), may hold values from 0.5 to 1.5
- query_weight: bfloat16 [16, 2048, 2048], P('client', None, 'tensor'), as said below
- key_weight: bfloat16 [16, 2048, 512], P('client', None, 'tensor'), as said below
- client_value_weight: bfloat16 [16, 2048, 512], P('client', None, 'tensor'), may hold values from -0.125 to 0.125
- output_weight: bfloat16 [16, 2048, 2048], P('client', None, 'tensor'), may hold values from -0.125 to 0.125
- server_gain: bfloat16 [2, 2048], P('sdata'), may hold values from 0.5 to 1.5
- server_gate: bfloat16 [2, 2048, 4096], P('sdata', None, 'tensor'), may hold values from -0.125 to 0.125
- server_up: bfloat16 [2, 2048, 4096], P('sdata', None, 'tensor'), may hold values from -0.125 to 0.125
- server_down: bfloat16 [2, 4096, 2048], P('sdata', 'tensor'), may hold values from -0.09375 to 0.09375
- upstream: bfloat16 [12288, 2048], P(('client', 'sdata')), may hold values from -6 to 6
- assignment: int32 [16], replicated, may hold values from 0 to 1, as said below
Outputs:
- query_update: bfloat16 [2048, 2048], P(('client', 'sdata'), 'tensor')
- key_update: bfloat16 [2048, 512], P(('client', 'sdata'), 'tensor')
- value_update: bfloat16 [2048, 512], P(('client', 'sdata'), 'tensor')
- output_update: bfloat16 [2048, 2048], P(('client', 'sdata'), 'tensor')
Inputs may be any that keep to these rules, and one draw needn't show every extreme that they name: `assignment`: each of the 2 server groups is named by exactly 8 clients. `query_weight`: independent entries with a spread of about 2048 ** -0.5. `key_weight`: entries with a spread of about 2048 ** -0.5 or more.
All inputs are finite; a program needn't handle non-finite values.
Results may differ from a plain program's by a relative error of at most 0.038.
The roundings to bfloat16 on the way count: a program that leaves them out, or rounds other values in their place, can miss the bound.
Values may be sent and summed in bfloat16 or wider, within the bound.
No kernel may reach another device: no remote copies, remote signals or barrier semaphores. Data moves between devices by JAX's collectives and lax.ppermute only.
A program may use at most 128 MiB of HBM per device.

v0:
```python
import jax
import jax.numpy as jnp
import numpy as np
from jax import lax
from jax.experimental import pallas as pl
from jax.experimental.pallas import tpu as pltpu
from jax.sharding import Mesh, PartitionSpec as P

HEAD_DIM = 64
HALF = HEAD_DIM // 2
BLOCK = 256
STRIP = 128
F32 = jnp.float32
BF16 = jnp.bfloat16
SMEM = pl.BlockSpec(memory_space=pltpu.SMEM)
VMEM = pl.BlockSpec(memory_space=pltpu.VMEM)


def on_core(kernel, outputs, scratch=()):
    def call(place, *operands):
        return pl.pallas_call(
            kernel,
            out_shape=[jax.ShapeDtypeStruct(shape, kind) for shape, kind in outputs],
            in_specs=[SMEM] + [VMEM] * len(operands),
            out_specs=[VMEM] * len(outputs),
            scratch_shapes=list(scratch),
            compiler_params=pltpu.CompilerParams(vmem_limit_bytes=60 * 1024 * 1024),
        )(place, *operands)

    return call


def dot(a, b):
    return jnp.dot(a, b, preferred_element_type=F32)


def dot_nt(a, b):
    return lax.dot_general(a, b, (((1,), (1,)), ((), ())), preferred_element_type=F32)


def dot_tn(a, b):
    return lax.dot_general(a, b, (((0,), (0,)), ((), ())), preferred_element_type=F32)


def rotary_tables(length):
    angles = np.arange(max(length // 16, 16))[:, None] * 500000.0 ** (-np.arange(HALF) * 2 / HEAD_DIM)
    wide = np.concatenate([angles] * 4, 1)
    fine, coarse = wide[:16], 16 * wide[: length // 16]
    return [np.float32(f(t)) for t in (fine, coarse) for f in (np.cos, np.sin)]


def expand_tables(fine_cos, fine_sin, coarse_cos, coarse_sin):
    near_cos, near_sin = fine_cos[...][None], fine_sin[...][None]
    far_cos, far_sin = coarse_cos[...][:, None], coarse_sin[...][:, None]
    shape = (far_cos.shape[0] * 16, far_cos.shape[2])
    cosine = (far_cos * near_cos - far_sin * near_sin).reshape(shape)
    sine = (far_sin * near_cos + far_cos * near_sin).reshape(shape)
    return cosine, sine


def first_half(shape):
    return lax.broadcasted_iota(jnp.int32, shape, 1) % HEAD_DIM < HALF


def ahead(value):
    return pltpu.roll(value, value.shape[1] - HALF, 1)


def behind(value):
    return pltpu.roll(value, HALF, 1)


def rotate(value, cosine, sine):
    turned = jnp.where(first_half(value.shape), -ahead(value), behind(value))
    return value * cosine + turned * sine


def rotate_back(grad, cosine, sine):
    scaled = grad * sine
    turned = jnp.where(first_half(grad.shape), ahead(scaled), -behind(scaled))
    return grad * cosine + turned


def block_start(core, x, offset):
    return pl.multiple_of((core * 4 + (x + offset) % 4) * BLOCK, BLOCK)


def attend_kernel(
    place, rows, gain, wq, wk, wv, wo, fine_cos, fine_sin, coarse_cos, coarse_sin,
    mine, other, own_input, normed, queries, keys, values, weights, context,
    parts,
):
    core, x = place[0], place[1]
    length, heads = rows.shape[0], queries.shape[0]
    gain_float = gain[...].astype(F32)

    @pl.loop(0, length // STRIP)
    def _(at):
        strip = pl.ds(pl.multiple_of(at * STRIP, STRIP), STRIP)
        rows_float = rows[strip, :].astype(F32)
        inv_rms = lax.rsqrt(jnp.mean(rows_float * rows_float, -1, keepdims=True) + 1e-05)
        normed[strip, :] = (rows_float * inv_rms * gain_float).astype(BF16)

    cos2, sin2 = expand_tables(fine_cos, fine_sin, coarse_cos, coarse_sin)
    cos4, sin4 = jnp.concatenate([cos2, cos2], 1), jnp.concatenate([sin2, sin2], 1)
    all_normed = normed[...]
    all_queries = rotate(dot(all_normed, wq[...]), cos4, sin4).astype(BF16)
    for head in range(heads):
        queries[head] = all_queries[:, head * HEAD_DIM : (head + 1) * HEAD_DIM]
    both = dot_nt(all_normed, jnp.concatenate([wk[...], wv[...]], 0))
    keys[...] = rotate(both, cos2, sin2)[:, :HEAD_DIM].astype(BF16)
    values[...] = both[:, HEAD_DIM:].astype(BF16)
    for at in range(0, length, STRIP):
        strip, seen = pl.ds(at, STRIP), at + STRIP
        shape = (STRIP, seen)
        allowed = lax.broadcasted_iota(jnp.int32, shape, 1) <= at + lax.broadcasted_iota(
            jnp.int32, shape, 0
        )

        @pl.loop(0, heads, unroll=4)
        def _(head):
            scores = dot_nt(queries[head, strip, :], keys[:seen, :]) * HEAD_DIM ** (-0.5)
            scores = jnp.where(allowed, scores, -1e30)
            exponent = jnp.exp(scores - jnp.max(scores, -1, keepdims=True))
            share = (exponent / jnp.sum(exponent, -1, keepdims=True)).astype(BF16)
            weights[head, strip, :seen] = share
            parts[head, strip, :] = dot(share, values[:seen, :])

    context[...] = jnp.concatenate([parts[head] for head in range(heads)], 1).astype(BF16)
    own_input[...] = rows[:, pl.ds(block_start(core, x, 0), BLOCK)]

    @pl.loop(0, 4)
    def _(step):
        there = wo[pl.ds(block_start(1 - core, x, step), BLOCK), :]
        other[step] = dot_nt(context[...], there).astype(BF16)
        here = wo[pl.ds(block_start(core, x, step), BLOCK), :]
        mine[step] = dot_nt(context[...], here).astype(BF16)


def spread(tall, y, targets):
    for step, target in enumerate(targets):
        there = (y + step) % 4

        @pl.loop(0, 8)
        def _(z):
            row = (((there % 2) * 8 + z) * 2 + there // 2) * 64
            target[z] = tall[pl.ds(pl.multiple_of(row, 64), 64), :]


def pull_kernel(place, kept, moved, kept_there, moved_there, down, pulled, own_upstream, whole):
    core, x = place[0], place[1]
    rows, wide = kept.shape
    sides = ((core, (kept, moved)), (1 - core, (kept_there, moved_there)))
    for side, halves in sides:
        for half, piece in enumerate(halves):
            start = pl.multiple_of(side * wide, wide)
            whole[pl.ds(half * rows, rows), pl.ds(start, wide)] = piece[...]
    own_upstream[...] = whole[:, pl.ds(block_start(core, x, 0), BLOCK)]
    pulled[...] = dot_nt(whole[...], down[...])


def server_kernel(
    place, p0, p1, p2, p3, q0, q1, pulled, gain, gate, up,
    mine, other, normed, grads, gates, ups, gate_grad, up_grad, inverse,
):
    core, x = place[0], place[1]
    pieces = (p0, p1, p2, p3, q0, q1.at[0], q1.at[1], q1.at[2])
    width, length = gate.shape[0], p0.shape[0]
    blocks = [
        pl.ds(block_start(core if index < 4 else 1 - core, x, 4 - index % 4), BLOCK)
        for index in range(8)
    ]

    def strips(step):
        @pl.loop(0, length // STRIP)
        def _(at):
            step(pl.ds(pl.multiple_of(at * STRIP, STRIP), STRIP))

    def normalize(strip):
        squares = jnp.zeros((STRIP, 1), F32)
        for piece in pieces:
            rows_float = piece[strip, :].astype(F32)
            squares = squares + jnp.sum(rows_float * rows_float, -1, keepdims=True)
        inv_rms = lax.rsqrt(squares / width + 1e-05)
        inverse[strip, :] = inv_rms
        for piece, some in zip(pieces, blocks):
            scaled = piece[strip, :].astype(F32) * inv_rms * gain[:, some].astype(F32)
            normed[strip, some] = scaled.astype(BF16)

    strips(normalize)
    gates[...] = dot(normed[...], gate[...])
    ups[...] = dot(normed[...], up[...])

    def through_gate(strip):
        gate_value, pull = gates[strip, :], pulled[strip, :]
        sigmoid_gate = jax.nn.sigmoid(gate_value)
        slope = sigmoid_gate * (1.0 + gate_value * (1.0 - sigmoid_gate))
        gate_grad[strip, :] = (pull * ups[strip, :] * slope).astype(BF16)
        up_grad[strip, :] = (pull * gate_value * sigmoid_gate).astype(BF16)

    strips(through_gate)
    for index, some in enumerate(blocks):
        grads[index] = dot_nt(gate_grad[...], gate[some, :]) + dot_nt(up_grad[...], up[some, :])

    def finish(strip):
        along = jnp.zeros((STRIP, 1), F32)
        for index, (piece, some) in enumerate(zip(pieces, blocks)):
            weighted = grads[index, strip, :] * gain[:, some].astype(F32)
            grads[index, strip, :] = weighted
            along = along + jnp.sum(weighted * piece[strip, :].astype(F32), -1, keepdims=True)
        inv_rms = inverse[strip, :]
        scale = inv_rms * inv_rms * inv_rms * (along / width)
        for index, piece in enumerate(pieces):
            part = inv_rms * grads[index, strip, :] - piece[strip, :].astype(F32) * scale
            step = (4 - index % 4) % 4
            if index < 4:
                mine[step, strip, :] = part.astype(BF16)
            else:
                other[step, strip, :] = part.astype(BF16)

    strips(finish)


def output_kernel(
    place, p0, p1, p2, p3, q0, q1, wo, context, context_grad, t0, t1, t2, t3, arrived, tall
):
    core, x = place[0], place[1]
    pieces = (p0, p1, p2, p3, q0, q1.at[0], q1.at[1], q1.at[2])
    for index, piece in enumerate(pieces):
        side = core if index < 4 else 1 - core
        some = pl.ds(block_start(side, x, 4 - index % 4), BLOCK)
        rows = piece[...]
        arrived[:, some] = rows
        tall[some, :] = dot_tn(rows, context[...]).astype(BF16)
    grads = dot(arrived[...], wo[...]).astype(BF16)
    for head in range(context_grad.shape[0]):
        context_grad[head] = grads[:, head * HEAD_DIM : (head + 1) * HEAD_DIM]
    spread(tall, place[2], (t0, t1, t2, t3))


def attend_back_kernel(
    place, context_grad, turned, queries, keys, values, weights, fine_cos, fine_sin, coarse_cos, coarse_sin,
    t0, t1, t2, t3, joined, tall, query_grad, key_grad, value_grad,
):
    heads, length = queries.shape[0], queries.shape[1]
    cos2, sin2 = expand_tables(fine_cos, fine_sin, coarse_cos, coarse_sin)
    cos4, sin4 = jnp.concatenate([cos2, cos2], 1), jnp.concatenate([sin2, sin2], 1)
    key_grad[...] = jnp.zeros_like(key_grad)
    value_grad[...] = jnp.zeros_like(value_grad)
    for at in range(0, length, STRIP):
        strip, seen = pl.ds(at, STRIP), at + STRIP

        @pl.loop(0, heads, unroll=2)
        def _(head):
            share, grads = weights[head, strip, :seen], context_grad[head, strip, :]
            share_float = share.astype(F32)
            share_grad = dot_nt(grads, values[:seen, :]).astype(BF16).astype(F32)
            level = jnp.sum(share_grad * share_float, -1, keepdims=True)
            score_grad = (share_float * (share_grad - level) * HEAD_DIM ** (-0.5)).astype(BF16)
            query_grad[head, strip, :] = dot(score_grad, keys[:seen, :])
            key_grad[:seen, :] += dot_tn(score_grad, queries[head, strip, :])
            value_grad[:seen, :] += dot_tn(share, grads)

    of_queries = jnp.concatenate([query_grad[head] for head in range(heads)], 1)
    joined[:, :BLOCK] = rotate_back(of_queries.astype(BF16).astype(F32), cos4, sin4).astype(BF16)
    pair = jnp.concatenate([key_grad[...], value_grad[...]], 1).astype(BF16).astype(F32)
    lane = lax.broadcasted_iota(jnp.int32, pair.shape, 1)
    back = jnp.where(lane < HEAD_DIM, rotate_back(pair, cos2, sin2), pair)
    joined[:, BLOCK:] = back.astype(BF16)
    tall[...] = dot(turned[...], joined[...]).astype(BF16)
    spread(tall, place[2], (t0, t1, t2, t3))


def x_shift(value, step):
    size = lax.axis_size("x")
    return lax.ppermute(value, "x", [(i, (i + step) % size) for i in range(size)])


def core_swap(value):
    return lax.ppermute(value, "core", [(0, 1), (1, 0)])


def group_swap(value):
    return lax.ppermute(value, "yh", [(0, 1), (1, 0)])


def y_shift(value, step):
    def place(y):
        return (y % 2) * 2 + y // 2

    return lax.ppermute(value, ("yl", "yh"), [(place(y), place((y + step) % 4)) for y in range(4)])


def over_clients(pieces):
    return lax.all_to_all(pieces, ("yl", "z"), 0, 0, tiled=True)


def pick(pieces, order):
    return pieces.at[order].get(mode="promise_in_bounds")


def added(*terms):
    return sum(term.astype(F32) for term in terms)


def relay_out(rows, order):
    pieces = over_clients(rows.reshape(16, -1, rows.shape[1]))
    arrived = group_swap(pick(pieces, order[8:]))
    return pieces, arrived


def relay_back(rows, inverse):
    pieces = rows.reshape(16, -1, BLOCK)
    returned = group_swap(pieces[8:])
    ordered = pick(jnp.concatenate([pieces[:8], returned], 0), inverse)
    return over_clients(ordered).reshape(rows.shape)


def share_sum(mine, other, *more):
    arrived = core_swap(other)
    pairs = [added(mine[step], arrived[step]) for step in range(4)]
    parts = [x_shift(pairs[step].astype(BF16), step) for step in (1, 3, 2)]
    return added(pairs[0], *parts, *more).astype(BF16)


def widen_rows(own):
    parts = [x_shift(own, step) for step in (1, 3, 2)]
    rest = [parts[0], parts[2], parts[1]]
    return [own, *rest, core_swap(own), core_swap(jnp.stack(rest))]


def tile_sum(tiles):
    parts = [y_shift(tiles[step], step) for step in (1, 3, 2)]
    summed = added(tiles[0], *parts).astype(BF16)
    pieces = lax.all_to_all(summed, "z", 0, 0, tiled=True)
    return (added(*pieces) / 16).astype(BF16)


def local(
    client_input,
    client_gain,
    query_weight,
    key_weight,
    client_value_weight,
    output_weight,
    server_gain,
    server_gate,
    server_up,
    server_down,
    upstream,
    assignment,
):
    length = client_input.shape[0]
    x, core, group = lax.axis_index("x"), lax.axis_index("core"), lax.axis_index("yh")
    at, y = jnp.arange(3), group * 2 + lax.axis_index("yl")
    place = jnp.where(at == 0, core, jnp.where(at == 1, x, y))
    leaves = (assignment != group).astype(jnp.int32)
    clients = jnp.arange(16)
    before = (clients[:, None] > clients[None, :]) & (leaves[:, None] == leaves[None, :])
    inverse = jnp.sum(before.astype(jnp.int32), 1) + 8 * leaves
    order = jnp.sum(jnp.where(inverse[None, :] == clients[:, None], clients[None, :], 0), 1)
    tables = rotary_tables(length)

    half = 4 * BLOCK
    own_upstream = lax.dynamic_slice_in_dim(upstream, core * half, half, 1)
    piece, stack = ((length, BLOCK), BF16), ((4, length, BLOCK), BF16)
    head = ((length, HEAD_DIM), BF16)
    heads = query_weight.shape[2] // HEAD_DIM
    by_head = ((heads, length, HEAD_DIM), BF16)
    fwd = on_core(
        attend_kernel,
        [stack, stack, piece, (client_input.shape, BF16), by_head, head, head]
        + [((heads, length, length), BF16), piece],
        [pltpu.VMEM((heads, length, HEAD_DIM), F32)],
    )(
        place, client_input, client_gain, query_weight[0], key_weight[0].T,
        client_value_weight[0].T, output_weight[0], *tables,
    )
    mine, other, (own_input, normed, queries, keys, values, weights, context) = (
        fwd[0], fwd[1], fwd[2:],
    )
    pieces, moved = relay_out(own_upstream, order)
    kept = pick(pieces, order[:8]).reshape(-1, half)
    moved = moved.reshape(-1, half)
    there = (core_swap(kept), core_swap(moved))
    pulled, server_upstream = on_core(
        pull_kernel,
        [((length, server_down.shape[1]), F32), piece],
        [pltpu.VMEM(client_input.shape, BF16)],
    )(place, kept, moved, *there, server_down[0])
    turned = normed.T
    pulled, turned = lax.optimization_barrier((pulled, turned))
    cut_input = share_sum(mine, other, own_input)
    pieces, moved = relay_out(cut_input, order)
    arranged = lax.dynamic_update_slice_in_dim(pick(pieces, order), moved, 8, 0)
    wide_rows = widen_rows(arranged.reshape(length, BLOCK))
    back = on_core(
        server_kernel,
        [stack, stack],
        [
            pltpu.VMEM(client_input.shape, BF16),
            pltpu.VMEM((8, length, BLOCK), F32),
            pltpu.VMEM((length, server_gate.shape[2]), F32),
            pltpu.VMEM((length, server_gate.shape[2]), F32),
            pltpu.VMEM((length, server_gate.shape[2]), BF16),
            pltpu.VMEM((length, server_gate.shape[2]), BF16),
            pltpu.VMEM((length, 1), F32),
        ],
    )(place, *wide_rows, pulled, server_gain, server_gate[0], server_up[0])
    cut_grad = share_sum(back[0], back[1], server_upstream)
    arriving = widen_rows(relay_back(cut_grad, inverse))
    width = client_input.shape[1]
    context_grad, *outs = on_core(
        output_kernel,
        [by_head] + [((8, 64, BLOCK), BF16)] * 4,
        [pltpu.VMEM(client_input.shape, BF16), pltpu.VMEM((width, BLOCK), BF16)],
    )(place, *arriving, output_weight[0], context)
    joined_width = BLOCK + 2 * HEAD_DIM
    tiles = on_core(
        attend_back_kernel,
        [((8, 64, joined_width), BF16)] * 4,
        [
            pltpu.VMEM((length, joined_width), BF16),
            pltpu.VMEM((width, joined_width), BF16),
            pltpu.VMEM((heads, length, HEAD_DIM), F32),
            pltpu.VMEM((length, HEAD_DIM), F32),
            pltpu.VMEM((length, HEAD_DIM), F32),
        ],
    )(place, context_grad, turned, queries, keys, values, weights, *tables)
    output_update = tile_sum(outs)
    total = tile_sum(tiles)
    return (
        total[:, :BLOCK],
        total[:, BLOCK : BLOCK + HEAD_DIM],
        total[:, BLOCK + HEAD_DIM :],
        output_update,
    )


def solution(mesh):
    fine = Mesh(mesh.devices.reshape(2, 8, 4, 2, 2), ("yl", "z", "x", "core", "yh"))
    client, tensor, sdata = ("yl", "z"), ("x", "core"), "yh"
    rows = ("yl", "z", "yh")
    placed = (
        P(rows, None),
        P(client, None),
        P(client, None, tensor),
        P(client, None, tensor),
        P(client, None, tensor),
        P(client, None, tensor),
        P(sdata, None),
        P(sdata, None, tensor),
        P(sdata, None, tensor),
        P(sdata, tensor, None),
        P(rows, None),
        P(),
    )
    return jax.shard_map(
        local,
        mesh=fine,
        in_specs=placed,
        out_specs=(P(rows, tensor), P(rows, tensor), P(rows, tensor), P(rows, tensor)),
        check_vma=False,
    )
```

profile of v0, /device:TPU:4, one launch (start us, length us, event | category | flops | bytes accessed | tf_op | source)
XLA Modules:
  0.0 219.8 jit_solution(13650193355004542396)
XLA Ops:
  1.2 10.8 %shard_map.183 = (bf16[4,384,256]{2,1,0:T(8,128)(2,1)}, bf16[4,384,256]{2,1,0:T(8,128)(2,1)}, bf16[384,256]{1,0:T(8,128)(2,1)}, bf16[384,2048]{1,0:T(8,128)(2,1)...) custom-call(s32[3]{0:T(128)} %compare_select_fusion.5.place, ...), custom_call_target="tpu_custom_call" | custom-call | tf_op jit(solution)/shard_map/pallas_call | solution.py:21
  20.1 5.1 %collective-permute-done.3 = bf16[384,256]{1,0:T(8,128)(2,1)S(1)} collective-permute-done((bf16[384,256]{1,0:T(8,128)(2,1)S(1)}, bf16[384,256]{1,0:T(8,128)(2,1)S(1)}, u32[]{:S(2)}, u32[]{:S(2)}) %collective-permute-start.3) | collective-permute-done | bytes 196640 | tf_op jit(solution)/shard_map/ppermute | solution.py:276
  30.3 9.6 %all-to-all-start = ((bf16[16,24,256]{2,1,0:T(8,128)(2,1)}), bf16[16,24,256]{2,1,0:T(8,128)(2,1)S(1)}, u32[]{:S(2)}, u32[]{:S(2)}) async-start(bf16[16,24,256]{2,1,0:T(8,128)(2,1)} %bitcast.10), calls=%async_computation | async-start | bytes 393216 | tf_op jit(solution)/shard_map/all_to_all | solution.py:295
  40.9 8.2 %all-to-all-done = bf16[16,24,256]{2,1,0:T(8,128)(2,1)S(1)} async-done(((bf16[16,24,256]{2,1,0:T(8,128)(2,1)}), bf16[16,24,256]{2,1,0:T(8,128)(2,1)S(1)}, u32[]{:S(2)}, u32[]{:S(2)}) %all-to-all-start) | async-done | bytes 196640 | tf_op jit(solution)/shard_map/all_to_all | solution.py:295
  49.1 4.2 %all-to-all-start.1 = ((bf16[16,24,1024]{2,1,0:T(8,128)(2,1)}), bf16[16,24,1024]{2,1,0:T(8,128)(2,1)S(1)}, u32[]{:S(2)}, u32[]{:S(2)}) async-start(bf16[16,24,1024]{2,1,0:T(8,128)(2,1)} %bitcast.17), calls=%async_computation.1 | async-start | bytes 1572864 | tf_op jit(solution)/shard_map/all_to_all | solution.py:295
  54.3 3.0 %collective-permute-start.4 = (bf16[8,24,256]{2,1,0:T(8,128)(2,1)S(1)}, bf16[8,24,256]{2,1,0:T(8,128)(2,1)S(1)}, u32[]{:S(2)}, u32[]{:S(2)}) collective-permute-start(bf16[8,24,256]{2,1,0:T(8,128)(2,1)S(1)} %gather_fusion.1), channel_id=1, source_target_pairs={{0,1},{1,0},{2,3},{3,2},{4,5},{5,4},{6,7},{7,6},{8,9},{9,8},{10,11... | collective-permute-start | bytes 294920 | tf_op jit(solution)/shard_map/ppermute | solution.py:284
  57.9 3.6 %collective-permute-done.4 = bf16[8,24,256]{2,1,0:T(8,128)(2,1)S(1)} collective-permute-done((bf16[8,24,256]{2,1,0:T(8,128)(2,1)S(1)}, bf16[8,24,256]{2,1,0:T(8,128)(2,1)S(1)}, u32[]{:S(2)}, u32[]{:S(2)}) %collective-permute-start.4) | collective-permute-done | bytes 98336 | tf_op jit(solution)/shard_map/ppermute | solution.py:284
  64.3 9.8 %all-to-all-done.1 = bf16[16,24,1024]{2,1,0:T(8,128)(2,1)S(1)} async-done(((bf16[16,24,1024]{2,1,0:T(8,128)(2,1)}), bf16[16,24,1024]{2,1,0:T(8,128)(2,1)S(1)}, u32[]{:S(2)}, u32[]{:S(2)}) %all-to-all-start.1) | async-done | bytes 786464 | tf_op jit(solution)/shard_map/all_to_all | solution.py:295
  75.4 2.9 %collective-permute-start.10 = (bf16[8,24,1024]{2,1,0:T(8,128)(2,1)}, bf16[8,24,1024]{2,1,0:T(8,128)(2,1)}, u32[]{:S(2)}, u32[]{:S(2)}) collective-permute-start(bf16[8,24,1024]{2,1,0:T(8,128)(2,1)} %gather_fusion.3), channel_id=1, source_target_pairs={{0,1},{1,0},{2,3},{3,2},{4,5},{5,4},{6,7},{7,6},{8,9},{9,8},{10,11... | collective-permute-start | bytes 1179656 | tf_op jit(solution)/shard_map/ppermute | solution.py:284
  80.6 5.9 %collective-permute-done.10 = bf16[8,24,1024]{2,1,0:T(8,128)(2,1)} collective-permute-done((bf16[8,24,1024]{2,1,0:T(8,128)(2,1)}, bf16[8,24,1024]{2,1,0:T(8,128)(2,1)}, u32[]{:S(2)}, u32[]{:S(2)}) %collective-permute-start.10) | collective-permute-done | bytes 393248 | tf_op jit(solution)/shard_map/ppermute | solution.py:284
  90.5 4.0 %shard_map.184 = (f32[384,512]{1,0:T(8,128)}, bf16[384,256]{1,0:T(8,128)(2,1)}) custom-call(s32[3]{0:T(128)} %compare_select_fusion.5.place, bf16[192,1024]{1,0:T(8,128)(2,1)} %bitcast.73, bf16[192,1024]{1,0:T(8,128)(2,1)} %bitcast.19.moved, bf16[192,1024]{1,0:T(8,128)(2,1)} %copy-done.12, bf16[192,1024]{1,0:T(8,128)(2,1)} %copy-done.13, ...), custom_call_target="tpu_custom_call" | custom-call | tf_op jit(solution)/shard_map/pallas_call | solution.py:21
  94.6 10.6 %shard_map.185 = (bf16[4,384,256]{2,1,0:T(8,128)(2,1)}, bf16[4,384,256]{2,1,0:T(8,128)(2,1)}) custom-call(s32[3]{0:T(128)} %compare_select_fusion.5.place, bf16[384,256]{1,0:T(8,128)(2,1)} %bitcast.90, bf16[384,256]{1,0:T(8,128)(2,1)} %copy-done.6, bf16[384,256]{1,0:T(8,128)(2,1)} %copy-done.7, bf16[384,256]{1,0:T(8,128)(2,1)} %copy-done.8, ...), custom_call_target="tpu_custom_call" | custom-call | tf_op jit(solution)/shard_map/pallas_call | solution.py:21
  111.7 6.6 %collective-permute-done.16 = bf16[384,256]{1,0:T(8,128)(2,1)S(1)} collective-permute-done((bf16[384,256]{1,0:T(8,128)(2,1)S(1)}, bf16[384,256]{1,0:T(8,128)(2,1)S(1)}, u32[]{:S(2)}, u32[]{:S(2)}) %collective-permute-start.16) | collective-permute-done | bytes 196640 | tf_op jit(solution)/shard_map/ppermute | solution.py:276
  122.8 3.0 %collective-permute-start.17 = (bf16[8,24,256]{2,1,0:T(8,128)(2,1)S(1)}, bf16[8,24,256]{2,1,0:T(8,128)(2,1)S(1)}, u32[]{:S(2)}, u32[]{:S(2)}) collective-permute-start(bf16[8,24,256]{2,1,0:T(8,128)(2,1)S(1)} %bitcast.94), channel_id=1, source_target_pairs={{0,1},{1,0},{2,3},{3,2},{4,5},{5,4},{6,7},{7,6},{8,9},{9,8},{10,11... | collective-permute-start | bytes 294920 | tf_op jit(solution)/shard_map/ppermute | solution.py:284
  125.8 3.3 %collective-permute-done.17 = bf16[8,24,256]{2,1,0:T(8,128)(2,1)S(1)} collective-permute-done((bf16[8,24,256]{2,1,0:T(8,128)(2,1)S(1)}, bf16[8,24,256]{2,1,0:T(8,128)(2,1)S(1)}, u32[]{:S(2)}, u32[]{:S(2)}) %collective-permute-start.17) | collective-permute-done | bytes 98336 | tf_op jit(solution)/shard_map/ppermute | solution.py:284
  129.7 15.1 %all_to_all.25 = bf16[16,24,256]{2,1,0:T(8,128)(2,1)S(1)} all-to-all(bf16[16,24,256]{2,1,0:T(8,128)(2,1)S(1)} %gather_fusion.4), channel_id=1, replica_groups=mesh['yl'=2,'z'=8,'x'=4,'core'=2,'yh'=2] {'yl','z'}, dimensions={0} | all-to-all | bytes 393216 | tf_op jit(solution)/shard_map/all_to_all | solution.py:295
  148.0 3.7 %collective-permute-done.18.p1 = bf16[384,256]{1,0:T(8,128)(2,1)S(1)} collective-permute-done((bf16[384,256]{1,0:T(8,128)(2,1)S(1)}, bf16[384,256]{1,0:T(8,128)(2,1)S(1)}, u32[]{:S(2)}, u32[]{:S(2)}) %collective-permute-start.18) | collective-permute-done | bytes 196640 | tf_op jit(solution)/shard_map/ppermute | solution.py:276
  158.7 4.7 %shard_map.186 = (bf16[4,384,64]{2,1,0:T(8,128)(2,1)}, bf16[8,64,256]{2,1,0:T(8,128)(2,1)}, bf16[8,64,256]{2,1,0:T(8,128)(2,1)}, bf16[8,64,256]{2,1,0:T(8,128)(2,1)}, bf16[8,64,256]{2,1,0:T(8,128)(2,1)}) custom-call(s32[3]{0:T(128)} %compare_select_fusion.5.place, bf16[384,256]{1,0:T(8,128)(2,1)} %bitcast.82, bf16[384,256]{1,0:T(8,128)(2,1)} %copy-done.2, ...), custom_call_target="tpu_custom_call" | custom-call | tf_op jit(solution)/shard_map/pallas_call | solution.py:21
  168.3 10.1 %shard_map.187 = (bf16[8,64,384]{2,1,0:T(8,128)(2,1)}, bf16[8,64,384]{2,1,0:T(8,128)(2,1)}, bf16[8,64,384]{2,1,0:T(8,128)(2,1)}, bf16[8,64,384]{2,1,0:T(8,128)(2,1)}) custom-call(s32[3]{0:T(128)} %compare_select_fusion.5.place, bf16[4,384,64]{2,1,0:T(8,128)(2,1)} %get-tuple-element.38.context_grad, bf16[2048,384]{1,0:T(8,128)(2,1)} %bitcast.66, ...), custom_call_target="tpu_custom_call" | custom-call | tf_op jit(solution)/shard_map/pallas_call | solution.py:21
  183.3 3.9 %all-to-all-start.4 = ((bf16[8,64,256]{2,1,0:T(8,128)(2,1)}), bf16[8,64,256]{2,1,0:T(8,128)(2,1)S(1)}, u32[]{:S(2)}, u32[]{:S(2)}) async-start(bf16[8,64,256]{2,1,0:T(8,128)(2,1)} %add_convert_fusion.1), calls=%async_computation.4 | async-start | bytes 524288 | tf_op jit(solution)/shard_map/all_to_all | solution.py:335
  187.2 4.9 %collective-permute-done.25 = bf16[8,64,384]{2,1,0:T(8,128)(2,1)S(1)} collective-permute-done((bf16[8,64,384]{2,1,0:T(8,128)(2,1)}, bf16[8,64,384]{2,1,0:T(8,128)(2,1)S(1)}, u32[]{:S(2)}, u32[]{:S(2)}) %collective-permute-start.25) | collective-permute-done | bytes 393248 | tf_op jit(solution)/shard_map/ppermute | solution.py:291
  192.1 6.2 %collective-permute-done.24 = bf16[8,64,384]{2,1,0:T(8,128)(2,1)S(1)} collective-permute-done((bf16[8,64,384]{2,1,0:T(8,128)(2,1)}, bf16[8,64,384]{2,1,0:T(8,128)(2,1)S(1)}, u32[]{:S(2)}, u32[]{:S(2)}) %collective-permute-start.24) | collective-permute-done | bytes 393248 | tf_op jit(solution)/shard_map/ppermute | solution.py:291
  199.8 3.8 %all-to-all-start.3 = ((bf16[8,64,384]{2,1,0:T(8,128)(2,1)}), bf16[8,64,384]{2,1,0:T(8,128)(2,1)S(1)}, u32[]{:S(2)}, u32[]{:S(2)}) async-start(bf16[8,64,384]{2,1,0:T(8,128)(2,1)} %add_convert_fusion), calls=%async_computation.3 | async-start | bytes 786432 | tf_op jit(solution)/shard_map/all_to_all | solution.py:335
  204.2 14.2 %all-to-all-done.3 = bf16[8,64,384]{2,1,0:T(8,128)(2,1)S(1)} async-done(((bf16[8,64,384]{2,1,0:T(8,128)(2,1)}), bf16[8,64,384]{2,1,0:T(8,128)(2,1)S(1)}, u32[]{:S(2)}, u32[]{:S(2)}) %all-to-all-start.3) | async-done | bytes 393248 | tf_op jit(solution)/shard_map/all_to_all | solution.py:335
  (119 shorter events, 61.7 us)
Async XLA Ops:
  15.8 9.4 %collective-permute-start.3 = (bf16[384,256]{1,0:T(8,128)(2,1)S(1)}, bf16[384,256]{1,0:T(8,128)(2,1)S(1)}, u32[]{:S(2)}, u32[]{:S(2)}) collective-permute-start(bf16[384,256]{1,0:T(8,128)(2,1)S(1)} %get-tuple-element.58), channel_id=1, source_target_pairs={{0,8},{4,12},{8,0},{12,4},{1,9},{5,13},{9,1},{13,5},{2,10},{6,14},... | collective-permute-start | bytes 589832 | tf_op jit(solution)/shard_map/ppermute | solution.py:276
  18.1 9.6 %collective-permute-start.2 = (bf16[384,256]{1,0:T(8,128)(2,1)S(1)}, bf16[384,256]{1,0:T(8,128)(2,1)S(1)}, u32[]{:S(2)}, u32[]{:S(2)}) collective-permute-start(bf16[384,256]{1,0:T(8,128)(2,1)S(1)} %get-tuple-element.59), channel_id=1, source_target_pairs={{0,12},{4,0},{8,4},{12,8},{1,13},{5,1},{9,5},{13,9},{2,14},{6,2},{... | collective-permute-start | bytes 589832 | tf_op jit(solution)/shard_map/ppermute | solution.py:276
  18.5 10.0 %collective-permute-start.1 = (bf16[384,256]{1,0:T(8,128)(2,1)S(1)}, bf16[384,256]{1,0:T(8,128)(2,1)S(1)}, u32[]{:S(2)}, u32[]{:S(2)}) collective-permute-start(bf16[384,256]{1,0:T(8,128)(2,1)S(1)} %get-tuple-element.57), channel_id=1, source_target_pairs={{0,4},{4,8},{8,12},{12,0},{1,5},{5,9},{9,13},{13,1},{2,6},{6,10},{... | collective-permute-start | bytes 589832 | tf_op jit(solution)/shard_map/ppermute | solution.py:276
  30.3 18.8 %all-to-all-start = ((bf16[16,24,256]{2,1,0:T(8,128)(2,1)}), bf16[16,24,256]{2,1,0:T(8,128)(2,1)S(1)}, u32[]{:S(2)}, u32[]{:S(2)}) async-start(bf16[16,24,256]{2,1,0:T(8,128)(2,1)} %bitcast.10), calls=%async_computation | async-start | bytes 393216 | tf_op jit(solution)/shard_map/all_to_all | solution.py:295
  49.1 25.0 %all-to-all-start.1 = ((bf16[16,24,1024]{2,1,0:T(8,128)(2,1)}), bf16[16,24,1024]{2,1,0:T(8,128)(2,1)S(1)}, u32[]{:S(2)}, u32[]{:S(2)}) async-start(bf16[16,24,1024]{2,1,0:T(8,128)(2,1)} %bitcast.17), calls=%async_computation.1 | async-start | bytes 1572864 | tf_op jit(solution)/shard_map/all_to_all | solution.py:295
  61.5 16.8 %collective-permute-start.5 = (bf16[384,256]{1,0:T(8,128)(2,1)S(1)}, bf16[384,256]{1,0:T(8,128)(2,1)S(1)}, u32[]{:S(2)}, u32[]{:S(2)}) collective-permute-start(bf16[384,256]{1,0:T(8,128)(2,1)S(1)} %bitcast.86), channel_id=1, source_target_pairs={{0,4},{4,8},{8,12},{12,0},{1,5},{5,9},{9,13},{13,1},{2,6},{6,10},{... | collective-permute-start | bytes 589832 | tf_op jit(solution)/shard_map/ppermute | solution.py:276
  62.8 15.6 %collective-permute-start.6 = (bf16[384,256]{1,0:T(8,128)(2,1)S(1)}, bf16[384,256]{1,0:T(8,128)(2,1)S(1)}, u32[]{:S(2)}, u32[]{:S(2)}) collective-permute-start(bf16[384,256]{1,0:T(8,128)(2,1)S(1)} %bitcast.87), channel_id=1, source_target_pairs={{0,8},{4,12},{8,0},{12,4},{1,9},{5,13},{9,1},{13,5},{2,10},{6,14},... | collective-permute-start | bytes 589832 | tf_op jit(solution)/shard_map/ppermute | solution.py:276
  63.6 14.8 %collective-permute-start.7 = (bf16[384,256]{1,0:T(8,128)(2,1)S(1)}, bf16[384,256]{1,0:T(8,128)(2,1)S(1)}, u32[]{:S(2)}, u32[]{:S(2)}) collective-permute-start(bf16[384,256]{1,0:T(8,128)(2,1)S(1)} %bitcast.88), channel_id=1, source_target_pairs={{0,12},{4,0},{8,4},{12,8},{1,13},{5,1},{9,5},{13,9},{2,14},{6,2},{... | collective-permute-start | bytes 589832 | tf_op jit(solution)/shard_map/ppermute | solution.py:276
  75.4 11.1 %collective-permute-start.10 = (bf16[8,24,1024]{2,1,0:T(8,128)(2,1)}, bf16[8,24,1024]{2,1,0:T(8,128)(2,1)}, u32[]{:S(2)}, u32[]{:S(2)}) collective-permute-start(bf16[8,24,1024]{2,1,0:T(8,128)(2,1)} %gather_fusion.3), channel_id=1, source_target_pairs={{0,1},{1,0},{2,3},{3,2},{4,5},{5,4},{6,7},{7,6},{8,9},{9,8},{10,11... | collective-permute-start | bytes 1179656 | tf_op jit(solution)/shard_map/ppermute | solution.py:284
  79.4 15.2 %collective-permute-start.9 = (bf16[3,384,256]{2,1,0:T(8,128)(2,1)}, bf16[3,384,256]{2,1,0:T(8,128)(2,1)}, u32[]{:S(2)}, u32[]{:S(2)}) collective-permute-start(bf16[3,384,256]{2,1,0:T(8,128)(2,1)} %pad_maximum_fusion), channel_id=1, source_target_pairs={{0,2},{2,0},{1,3},{3,1},{4,6},{6,4},{5,7},{7,5},{8,10},{10,8},{9,1... | collective-permute-start | bytes 1769480 | tf_op jit(solution)/shard_map/ppermute | solution.py:280
  80.0 9.6 %collective-permute-start.11 = (bf16[192,1024]{1,0:T(8,128)(2,1)S(1)}, bf16[192,1024]{1,0:T(8,128)(2,1)S(1)}, u32[]{:S(2)}, u32[]{:S(2)}) collective-permute-start(bf16[192,1024]{1,0:T(8,128)(2,1)S(1)} %bitcast.72), channel_id=1, source_target_pairs={{0,2},{2,0},{1,3},{3,1},{4,6},{6,4},{5,7},{7,5},{8,10},{10,8},{9,1... | collective-permute-start | bytes 1179656 | tf_op jit(solution)/shard_map/ppermute | solution.py:280
  86.5 8.1 %collective-permute-start.8 = (bf16[384,256]{1,0:T(8,128)(2,1)S(1)}, bf16[384,256]{1,0:T(8,128)(2,1)}, u32[]{:S(2)}, u32[]{:S(2)}) collective-permute-start(bf16[384,256]{1,0:T(8,128)(2,1)S(1)} %bitcast.89), channel_id=1, source_target_pairs={{0,2},{2,0},{1,3},{3,1},{4,6},{6,4},{5,7},{7,5},{8,10},{10,8},{9,1... | collective-permute-start | bytes 589832 | tf_op jit(solution)/shard_map/ppermute | solution.py:280
  109.0 9.4 %collective-permute-start.16 = (bf16[384,256]{1,0:T(8,128)(2,1)S(1)}, bf16[384,256]{1,0:T(8,128)(2,1)S(1)}, u32[]{:S(2)}, u32[]{:S(2)}) collective-permute-start(bf16[384,256]{1,0:T(8,128)(2,1)S(1)} %get-tuple-element.55), channel_id=1, source_target_pairs={{0,8},{4,12},{8,0},{12,4},{1,9},{5,13},{9,1},{13,5},{2,10},{6,14},... | collective-permute-start | bytes 589832 | tf_op jit(solution)/shard_map/ppermute | solution.py:276
  109.1 11.7 %collective-permute-start.15 = (bf16[384,256]{1,0:T(8,128)(2,1)S(1)}, bf16[384,256]{1,0:T(8,128)(2,1)S(1)}, u32[]{:S(2)}, u32[]{:S(2)}) collective-permute-start(bf16[384,256]{1,0:T(8,128)(2,1)S(1)} %get-tuple-element.56), channel_id=1, source_target_pairs={{0,12},{4,0},{8,4},{12,8},{1,13},{5,1},{9,5},{13,9},{2,14},{6,2},{... | collective-permute-start | bytes 589832 | tf_op jit(solution)/shard_map/ppermute | solution.py:276
  111.7 10.0 %collective-permute-start.14 = (bf16[384,256]{1,0:T(8,128)(2,1)S(1)}, bf16[384,256]{1,0:T(8,128)(2,1)S(1)}, u32[]{:S(2)}, u32[]{:S(2)}) collective-permute-start(bf16[384,256]{1,0:T(8,128)(2,1)S(1)} %get-tuple-element.54), channel_id=1, source_target_pairs={{0,4},{4,8},{8,12},{12,0},{1,5},{5,9},{9,13},{13,1},{2,6},{6,10},{... | collective-permute-start | bytes 589832 | tf_op jit(solution)/shard_map/ppermute | solution.py:276
  146.9 8.4 %collective-permute-start.20 = (bf16[384,256]{1,0:T(8,128)(2,1)S(1)}, bf16[384,256]{1,0:T(8,128)(2,1)S(1)}, u32[]{:S(2)}, u32[]{:S(2)}) collective-permute-start(bf16[384,256]{1,0:T(8,128)(2,1)S(1)} %bitcast.80), channel_id=1, source_target_pairs={{0,12},{4,0},{8,4},{12,8},{1,13},{5,1},{9,5},{13,9},{2,14},{6,2},{... | collective-permute-start | bytes 589832 | tf_op jit(solution)/shard_map/ppermute | solution.py:276
  163.3 18.2 %collective-permute-start.28 = (bf16[8,64,256]{2,1,0:T(8,128)(2,1)}, bf16[8,64,256]{2,1,0:T(8,128)(2,1)S(1)}, u32[]{:S(2)}, u32[]{:S(2)}) collective-permute-start(bf16[8,64,256]{2,1,0:T(8,128)(2,1)} %get-tuple-element.51), channel_id=1, source_target_pairs={{0,1},{128,129},{1,0},{129,128},{2,3},{130,131},{3,2},{131,130},{4... | collective-permute-start | bytes 786440 | tf_op jit(solution)/shard_map/ppermute | solution.py:291
  166.2 15.3 %collective-permute-start.27 = (bf16[8,64,256]{2,1,0:T(8,128)(2,1)}, bf16[8,64,256]{2,1,0:T(8,128)(2,1)S(1)}, u32[]{:S(2)}, u32[]{:S(2)}) collective-permute-start(bf16[8,64,256]{2,1,0:T(8,128)(2,1)} %get-tuple-element.50), channel_id=1, source_target_pairs={{0,129},{128,0},{1,128},{129,1},{2,131},{130,2},{3,130},{131,3},{4... | collective-permute-start | bytes 786440 | tf_op jit(solution)/shard_map/ppermute | solution.py:291
  167.1 14.4 %collective-permute-start.26 = (bf16[8,64,256]{2,1,0:T(8,128)(2,1)}, bf16[8,64,256]{2,1,0:T(8,128)(2,1)}, u32[]{:S(2)}, u32[]{:S(2)}) collective-permute-start(bf16[8,64,256]{2,1,0:T(8,128)(2,1)} %get-tuple-element.49), channel_id=1, source_target_pairs={{0,128},{128,1},{1,129},{129,0},{2,130},{130,3},{3,131},{131,2},{4... | collective-permute-start | bytes 786440 | tf_op jit(solution)/shard_map/ppermute | solution.py:291
  178.3 13.8 %collective-permute-start.25 = (bf16[8,64,384]{2,1,0:T(8,128)(2,1)}, bf16[8,64,384]{2,1,0:T(8,128)(2,1)S(1)}, u32[]{:S(2)}, u32[]{:S(2)}) collective-permute-start(bf16[8,64,384]{2,1,0:T(8,128)(2,1)} %get-tuple-element.47), channel_id=1, source_target_pairs={{0,1},{128,129},{1,0},{129,128},{2,3},{130,131},{3,2},{131,130},{4... | collective-permute-start | bytes 1179656 | tf_op jit(solution)/shard_map/ppermute | solution.py:291
  179.0 19.3 %collective-permute-start.24 = (bf16[8,64,384]{2,1,0:T(8,128)(2,1)}, bf16[8,64,384]{2,1,0:T(8,128)(2,1)S(1)}, u32[]{:S(2)}, u32[]{:S(2)}) collective-permute-start(bf16[8,64,384]{2,1,0:T(8,128)(2,1)} %get-tuple-element.46), channel_id=1, source_target_pairs={{0,129},{128,0},{1,128},{129,1},{2,131},{130,2},{3,130},{131,3},{4... | collective-permute-start | bytes 1179656 | tf_op jit(solution)/shard_map/ppermute | solution.py:291
  181.5 17.3 %collective-permute-start.23 = (bf16[8,64,384]{2,1,0:T(8,128)(2,1)}, bf16[8,64,384]{2,1,0:T(8,128)(2,1)S(1)}, u32[]{:S(2)}, u32[]{:S(2)}) collective-permute-start(bf16[8,64,384]{2,1,0:T(8,128)(2,1)} %get-tuple-element.45), channel_id=1, source_target_pairs={{0,128},{128,1},{1,129},{129,0},{2,130},{130,3},{3,131},{131,2},{4... | collective-permute-start | bytes 1179656 | tf_op jit(solution)/shard_map/ppermute | solution.py:291
  183.3 16.5 %all-to-all-start.4 = ((bf16[8,64,256]{2,1,0:T(8,128)(2,1)}), bf16[8,64,256]{2,1,0:T(8,128)(2,1)S(1)}, u32[]{:S(2)}, u32[]{:S(2)}) async-start(bf16[8,64,256]{2,1,0:T(8,128)(2,1)} %add_convert_fusion.1), calls=%async_computation.4 | async-start | bytes 524288 | tf_op jit(solution)/shard_map/all_to_all | solution.py:335
  199.8 18.7 %all-to-all-start.3 = ((bf16[8,64,384]{2,1,0:T(8,128)(2,1)}), bf16[8,64,384]{2,1,0:T(8,128)(2,1)S(1)}, u32[]{:S(2)}, u32[]{:S(2)}) async-start(bf16[8,64,384]{2,1,0:T(8,128)(2,1)} %add_convert_fusion), calls=%async_computation.3 | async-start | bytes 786432 | tf_op jit(solution)/shard_map/all_to_all | solution.py:335
  (28 other events, 260.5 us)
where the time goes:
time: 222 us; the launch traced here: 220 us
  waiting for transfers between devices  89.1 us (40%)
  starting transfers between devices  53.2 us (24%)
  Pallas kernels  40.2 us (18%)
  blocking collectives  15.1 us (7%)
  other arithmetic  10.9 us (5%)
  local copies, waits for them, and re-layouts  10.3 us (5%)
    pallas_call x5, Pallas kernels, call(): pl.pallas_call(kernel, out_shape=[jax.ShapeDtypeStruct(shape, kind) for s...  40.2 us
    ppermute x12, waiting for transfers between devices, x_shift(): lax.ppermute(value, 'x', [(i, (i + step) % size) for i in range(size)])  25.7 us
    all_to_all x2, waiting for transfers between devices, over_clients(): return lax.all_to_all(pieces, ('yl', 'z'), 0, 0, tiled=True)  18 us
    all_to_all x1, blocking collectives, over_clients(): return lax.all_to_all(pieces, ('yl', 'z'), 0, 0, tiled=True)  15.1 us
    all_to_all x2, waiting for transfers between devices, tile_sum(): pieces = lax.all_to_all(summed, 'z', 0, 0, tiled=True)  14.2 us
    all_to_all x2, starting transfers between devices, over_clients(): return lax.all_to_all(pieces, ('yl', 'z'), 0, 0, tiled=True)  13.7 us
    ppermute x12, starting transfers between devices, x_shift(): lax.ppermute(value, 'x', [(i, (i + step) % size) for i in range(size)])  13 us
    ppermute x3, waiting for transfers between devices, group_swap(): return lax.ppermute(value, 'yh', [(0, 1), (1, 0)])  12.8 us
  transfers between devices with their start and end apart: 33, of which 21 were waited for; matrix products, arithmetic and copies ran while one was open for 5% of the time, Pallas kernels for 6%

commit v1 on v0

--- a/solution.py
+++ b/solution.py
@@ -16,15 +16,43 @@
 VMEM = pl.BlockSpec(memory_space=pltpu.VMEM)
 
 
-def on_core(kernel, outputs, scratch=()):
+ANY = pl.BlockSpec(memory_space=pl.ANY)
+
+
+class Late:
+    def __init__(self, source, target, semaphore):
+        self.copy, self.target = pltpu.make_async_copy(source, target, semaphore), target
+        self.copy.start()
+
+    def ready(self):
+        self.copy.wait()
+        return self.target
+
+
+def on_core(kernel, outputs, scratch=(), late=(), limit=24):
     def call(place, *operands):
+        count = len(operands)
+        kept = count + len(outputs) + len(scratch)
+
+        def body(place, *refs):
+            semaphores = refs[-1]
+            values = list(refs[:count])
+            for at, index in enumerate(late):
+                values[index] = Late(refs[index], refs[kept + at], semaphores.at[at])
+            kernel(place, *values, *refs[count:kept])
+
+        buffers = [pltpu.VMEM(operands[index].shape, operands[index].dtype) for index in late]
         return pl.pallas_call(
-            kernel,
+            body,
             out_shape=[jax.ShapeDtypeStruct(shape, kind) for shape, kind in outputs],
-            in_specs=[SMEM] + [VMEM] * len(operands),
+            in_specs=[SMEM] + [ANY if index in late else VMEM for index in range(count)],
             out_specs=[VMEM] * len(outputs),
-            scratch_shapes=list(scratch),
-            compiler_params=pltpu.CompilerParams(vmem_limit_bytes=60 * 1024 * 1024),
+            scratch_shapes=[
+                *scratch,
+                *buffers,
+                pltpu.SemaphoreType.DMA((max(len(late), 1),)),
+            ],
+            compiler_params=pltpu.CompilerParams(vmem_limit_bytes=limit * 1024 * 1024),
         )(place, *operands)
 
     return call
@@ -81,25 +109,28 @@
     return grad * cosine + turned
 
 
+def normalize(rows, gain, strip):
+    rows_float = rows[strip, :].astype(F32)
+    inv_rms = lax.rsqrt(jnp.mean(rows_float * rows_float, -1, keepdims=True) + 1e-05)
+    return (rows_float * inv_rms * gain[...].astype(F32)).astype(BF16)
+
+
 def block_start(core, x, offset):
     return pl.multiple_of((core * 4 + (x + offset) % 4) * BLOCK, BLOCK)
 
 
 def attend_kernel(
     place, rows, gain, wq, wk, wv, wo, fine_cos, fine_sin, coarse_cos, coarse_sin,
-    mine, other, own_input, normed, queries, keys, values, weights, context,
-    parts,
+    mine, other, own_input, queries, keys, values, weights, context,
+    parts, normed,
 ):
     core, x = place[0], place[1]
-    length, heads = rows.shape[0], queries.shape[0]
-    gain_float = gain[...].astype(F32)
+    length, heads = normed.shape[0], queries.shape[0]
 
     @pl.loop(0, length // STRIP)
     def _(at):
         strip = pl.ds(pl.multiple_of(at * STRIP, STRIP), STRIP)
-        rows_float = rows[strip, :].astype(F32)
-        inv_rms = lax.rsqrt(jnp.mean(rows_float * rows_float, -1, keepdims=True) + 1e-05)
-        normed[strip, :] = (rows_float * inv_rms * gain_float).astype(BF16)
+        normed[strip, :] = normalize(rows, gain, strip)
 
     cos2, sin2 = expand_tables(fine_cos, fine_sin, coarse_cos, coarse_sin)
     cos4, sin4 = jnp.concatenate([cos2, cos2], 1), jnp.concatenate([sin2, sin2], 1)
@@ -147,7 +178,7 @@
             target[z] = tall[pl.ds(pl.multiple_of(row, 64), 64), :]
 
 
-def pull_kernel(place, kept, moved, kept_there, moved_there, down, pulled, own_upstream, whole):
+def pull_kernel(place, kept, moved, kept_there, moved_there, down, client_rows, gain, pulled, own_upstream, turned, whole):
     core, x = place[0], place[1]
     rows, wide = kept.shape
     sides = ((core, (kept, moved)), (1 - core, (kept_there, moved_there)))
@@ -156,7 +187,10 @@
             start = pl.multiple_of(side * wide, wide)
             whole[pl.ds(half * rows, rows), pl.ds(start, wide)] = piece[...]
     own_upstream[...] = whole[:, pl.ds(block_start(core, x, 0), BLOCK)]
-    pulled[...] = dot_nt(whole[...], down[...])
+    pulled[...] = dot_nt(whole[...], down.ready()[...])
+    client_rows = client_rows.ready()
+    for at in range(0, whole.shape[0], STRIP):
+        turned[:, at : at + STRIP] = normalize(client_rows, gain, pl.ds(at, STRIP)).T
 
 
 def server_kernel(
@@ -165,7 +199,7 @@
 ):
     core, x = place[0], place[1]
     pieces = (p0, p1, p2, p3, q0, q1.at[0], q1.at[1], q1.at[2])
-    width, length = gate.shape[0], p0.shape[0]
+    width, length = normed.shape[1], p0.shape[0]
     blocks = [
         pl.ds(block_start(core if index < 4 else 1 - core, x, 4 - index % 4), BLOCK)
         for index in range(8)
@@ -188,7 +222,9 @@
             normed[strip, some] = scaled.astype(BF16)
 
     strips(normalize)
+    gate = gate.ready()
     gates[...] = dot(normed[...], gate[...])
+    up = up.ready()
     ups[...] = dot(normed[...], up[...])
 
     def through_gate(strip):
@@ -369,27 +405,28 @@
     by_head = ((heads, length, HEAD_DIM), BF16)
     fwd = on_core(
         attend_kernel,
-        [stack, stack, piece, (client_input.shape, BF16), by_head, head, head]
+        [stack, stack, piece, by_head, head, head]
         + [((heads, length, length), BF16), piece],
-        [pltpu.VMEM((heads, length, HEAD_DIM), F32)],
+        [pltpu.VMEM((heads, length, HEAD_DIM), F32), pltpu.VMEM(client_input.shape, BF16)],
+        limit=60,
     )(
         place, client_input, client_gain, query_weight[0], key_weight[0].T,
         client_value_weight[0].T, output_weight[0], *tables,
     )
-    mine, other, (own_input, normed, queries, keys, values, weights, context) = (
+    mine, other, (own_input, queries, keys, values, weights, context) = (
         fwd[0], fwd[1], fwd[2:],
     )
     pieces, moved = relay_out(own_upstream, order)
     kept = pick(pieces, order[:8]).reshape(-1, half)
     moved = moved.reshape(-1, half)
     there = (core_swap(kept), core_swap(moved))
-    pulled, server_upstream = on_core(
+    pulled, server_upstream, turned = on_core(
         pull_kernel,
-        [((length, server_down.shape[1]), F32), piece],
+        [((length, server_down.shape[1]), F32), piece, (client_input.shape[::-1], BF16)],
         [pltpu.VMEM(client_input.shape, BF16)],
-    )(place, kept, moved, *there, server_down[0])
-    turned = normed.T
-    pulled, turned = lax.optimization_barrier((pulled, turned))
+        late=(4, 5),
+        limit=60,
+    )(place, kept, moved, *there, server_down[0], client_input, client_gain)
     cut_input = share_sum(mine, other, own_input)
     pieces, moved = relay_out(cut_input, order)
     arranged = lax.dynamic_update_slice_in_dim(pick(pieces, order), moved, 8, 0)
@@ -406,6 +443,8 @@
             pltpu.VMEM((length, server_gate.shape[2]), BF16),
             pltpu.VMEM((length, 1), F32),
         ],
+        late=(8, 9),
+        limit=60,
     )(place, *wide_rows, pulled, server_gain, server_gate[0], server_up[0])
     cut_grad = share_sum(back[0], back[1], server_upstream)
     arriving = widen_rows(relay_back(cut_grad, inverse))

time: 222 us -> 212 us (0.955)
  waiting for transfers between devices: 89.1 us -> 76.1 us
  starting transfers between devices: 53.2 us -> 63.3 us
  Pallas kernels: 40.2 us -> 35.9 us
  local copies, waits for them, and re-layouts: 10.3 us -> 7.38 us
    ppermute x12, starting transfers between devices: 13 us -> 22.5 us  [x_shift(): lax.ppermute(value, 'x', [(i, (i + step) % size) for i in range(size)])]
    ppermute x12, waiting for transfers between devices: 25.7 us -> 18.5 us  [x_shift(): lax.ppermute(value, 'x', [(i, (i + step) % size) for i in range(size)])]
    pallas_call x5, Pallas kernels: 40.2 us -> 35.9 us  [call(): pl.pallas_call(body, out_shape=[jax.ShapeDtypeStruct(shape, kind) for sha...]
    all_to_all x2, waiting for transfers between devices: 18 us -> 14.5 us  [over_clients(): return lax.all_to_all(pieces, ('yl', 'z'), 0, 0, tiled=True)]
    pallas_call x1 -> x0, local copies, waits for them, and re-layouts: 2.59 us -> none  [call(): pl.pallas_call(kernel, out_shape=[jax.ShapeDtypeStruct(shape, kind) for s...]
    ppermute x3, waiting for transfers between devices: 12.8 us -> 10.6 us  [group_swap(): return lax.ppermute(value, 'yh', [(0, 1), (1, 0)])]
  transfers between devices with their start and end apart: 33 -> 33, of which waited for: 21 -> 19; matrix products, arithmetic and copies ran while one was open for 5% -> 4% of each run, Pallas kernels for 6% -> 6%
where the time goes in v1:
time: 212 us; the launch traced here: 210 us
  waiting for transfers between devices  76.1 us (36%)
  starting transfers between devices  63.3 us (30%)
  Pallas kernels  35.9 us (17%)
  blocking collectives  14.5 us (7%)
  other arithmetic  11.1 us (5%)
  local copies, waits for them, and re-layouts  7.38 us (3%)
    pallas_call x5, Pallas kernels, call(): pl.pallas_call(body, out_shape=[jax.ShapeDtypeStruct(shape, kind) for sha...  35.9 us
    ppermute x12, starting transfers between devices, x_shift(): lax.ppermute(value, 'x', [(i, (i + step) % size) for i in range(size)])  22.5 us
    ppermute x12, waiting for transfers between devices, x_shift(): lax.ppermute(value, 'x', [(i, (i + step) % size) for i in range(size)])  18.5 us
    all_to_all x1, blocking collectives, over_clients(): return lax.all_to_all(pieces, ('yl', 'z'), 0, 0, tiled=True)  14.5 us
    all_to_all x2, waiting for transfers between devices, over_clients(): return lax.all_to_all(pieces, ('yl', 'z'), 0, 0, tiled=True)  14.5 us
    all_to_all x2, waiting for transfers between devices, tile_sum(): pieces = lax.all_to_all(summed, 'z', 0, 0, tiled=True)  13.4 us
    all_to_all x2, starting transfers between devices, over_clients(): return lax.all_to_all(pieces, ('yl', 'z'), 0, 0, tiled=True)  12.8 us
    ppermute x6, waiting for transfers between devices, y_shift(): lax.ppermute(value, ('yl', 'yh'), [(place(y), place((y + step) % 4)) for...  11.2 us
  transfers between devices with their start and end apart: 33, of which 19 were waited for; matrix products, arithmetic and copies ran while one was open for 4% of the time, Pallas kernels for 6%

profile of v1, /device:TPU:4, one launch (start us, length us, event | category | flops | bytes accessed | tf_op | source)
XLA Modules:
  0.0 209.5 jit_solution(16021539215287591424)
XLA Ops:
  1.2 10.2 %shard_map.183 = (bf16[4,384,256]{2,1,0:T(8,128)(2,1)}, bf16[4,384,256]{2,1,0:T(8,128)(2,1)}, bf16[384,256]{1,0:T(8,128)(2,1)}, bf16[4,384,64]{2,1,0:T(8,128)(2,...) custom-call(s32[3]{0:T(128)} %compare_select_fusion.5.place, ...), custom_call_target="tpu_custom_call" | custom-call | tf_op jit(solution)/shard_map/pallas_call | solution.py:45
  17.3 3.4 %collective-permute-start.3 = (bf16[384,256]{1,0:T(8,128)(2,1)S(1)}, bf16[384,256]{1,0:T(8,128)(2,1)S(1)}, u32[]{:S(2)}, u32[]{:S(2)}) collective-permute-start(bf16[384,256]{1,0:T(8,128)(2,1)S(1)} %get-tuple-element.54), channel_id=1, source_target_pairs={{0,8},{4,12},{8,0},{12,4},{1,9},{5,13},{9,1},{13,5},{2,10},{6,14},... | collective-permute-start | bytes 589832 | tf_op jit(solution)/shard_map/ppermute | solution.py:312
  28.7 9.1 %all-to-all-start = ((bf16[16,24,256]{2,1,0:T(8,128)(2,1)}), bf16[16,24,256]{2,1,0:T(8,128)(2,1)S(1)}, u32[]{:S(2)}, u32[]{:S(2)}) async-start(bf16[16,24,256]{2,1,0:T(8,128)(2,1)} %bitcast.10), calls=%async_computation | async-start | bytes 393216 | tf_op jit(solution)/shard_map/all_to_all | solution.py:331
  38.8 8.0 %all-to-all-done = bf16[16,24,256]{2,1,0:T(8,128)(2,1)S(1)} async-done(((bf16[16,24,256]{2,1,0:T(8,128)(2,1)}), bf16[16,24,256]{2,1,0:T(8,128)(2,1)S(1)}, u32[]{:S(2)}, u32[]{:S(2)}) %all-to-all-start) | async-done | bytes 196640 | tf_op jit(solution)/shard_map/all_to_all | solution.py:331
  46.8 3.7 %all-to-all-start.1 = ((bf16[16,24,1024]{2,1,0:T(8,128)(2,1)}), bf16[16,24,1024]{2,1,0:T(8,128)(2,1)S(1)}, u32[]{:S(2)}, u32[]{:S(2)}) async-start(bf16[16,24,1024]{2,1,0:T(8,128)(2,1)} %bitcast.17), calls=%async_computation.1 | async-start | bytes 1572864 | tf_op jit(solution)/shard_map/all_to_all | solution.py:331
  51.5 3.0 %collective-permute-start.4 = (bf16[8,24,256]{2,1,0:T(8,128)(2,1)S(1)}, bf16[8,24,256]{2,1,0:T(8,128)(2,1)S(1)}, u32[]{:S(2)}, u32[]{:S(2)}) collective-permute-start(bf16[8,24,256]{2,1,0:T(8,128)(2,1)S(1)} %gather_fusion.1), channel_id=1, source_target_pairs={{0,1},{1,0},{2,3},{3,2},{4,5},{5,4},{6,7},{7,6},{8,9},{9,8},{10,11... | collective-permute-start | bytes 294920 | tf_op jit(solution)/shard_map/ppermute | solution.py:320
  55.0 3.0 %collective-permute-done.4 = bf16[8,24,256]{2,1,0:T(8,128)(2,1)S(1)} collective-permute-done((bf16[8,24,256]{2,1,0:T(8,128)(2,1)S(1)}, bf16[8,24,256]{2,1,0:T(8,128)(2,1)S(1)}, u32[]{:S(2)}, u32[]{:S(2)}) %collective-permute-start.4) | collective-permute-done | bytes 98336 | tf_op jit(solution)/shard_map/ppermute | solution.py:320
  58.0 3.9 %collective-permute-start.5 = (bf16[384,256]{1,0:T(8,128)(2,1)S(1)}, bf16[384,256]{1,0:T(8,128)(2,1)S(1)}, u32[]{:S(2)}, u32[]{:S(2)}) collective-permute-start(bf16[384,256]{1,0:T(8,128)(2,1)S(1)} %bitcast.84), channel_id=1, source_target_pairs={{0,4},{4,8},{8,12},{12,0},{1,5},{5,9},{9,13},{13,1},{2,6},{6,10},{... | collective-permute-start | bytes 589832 | tf_op jit(solution)/shard_map/ppermute | solution.py:312
  63.5 6.5 %all-to-all-done.1 = bf16[16,24,1024]{2,1,0:T(8,128)(2,1)S(1)} async-done(((bf16[16,24,1024]{2,1,0:T(8,128)(2,1)}), bf16[16,24,1024]{2,1,0:T(8,128)(2,1)S(1)}, u32[]{:S(2)}, u32[]{:S(2)}) %all-to-all-start.1) | async-done | bytes 786464 | tf_op jit(solution)/shard_map/all_to_all | solution.py:331
  71.3 2.9 %collective-permute-start.10 = (bf16[8,24,1024]{2,1,0:T(8,128)(2,1)}, bf16[8,24,1024]{2,1,0:T(8,128)(2,1)}, u32[]{:S(2)}, u32[]{:S(2)}) collective-permute-start(bf16[8,24,1024]{2,1,0:T(8,128)(2,1)} %gather_fusion.3), channel_id=1, source_target_pairs={{0,1},{1,0},{2,3},{3,2},{4,5},{5,4},{6,7},{7,6},{8,9},{9,8},{10,11... | collective-permute-start | bytes 1179656 | tf_op jit(solution)/shard_map/ppermute | solution.py:320
  76.5 4.5 %collective-permute-done.10 = bf16[8,24,1024]{2,1,0:T(8,128)(2,1)} collective-permute-done((bf16[8,24,1024]{2,1,0:T(8,128)(2,1)}, bf16[8,24,1024]{2,1,0:T(8,128)(2,1)}, u32[]{:S(2)}, u32[]{:S(2)}) %collective-permute-start.10) | collective-permute-done | bytes 393248 | tf_op jit(solution)/shard_map/ppermute | solution.py:320
  83.7 5.9 %shard_map.184 = (f32[384,512]{1,0:T(8,128)}, bf16[384,256]{1,0:T(8,128)(2,1)}, bf16[2048,384]{1,0:T(8,128)(2,1)}) custom-call(s32[3]{0:T(128)} %compare_select_fusion.5.place, bf16[192,1024]{1,0:T(8,128)(2,1)} %bitcast.79, bf16[192,1024]{1,0:T(8,128)(2,1)} %bitcast.19.refs_1_, bf16[192,1024]{1,0:T(8,128)(2,1)} %copy-done.18, bf16[192,1024]{1,0:T(8,128)(2,1)} %copy-done.19, ...), custom_call_target="tpu_custom_call" | custom-call | tf_op jit(solution)/shard_map/pallas_call | solution.py:45
  90.3 10.0 %shard_map.185 = (bf16[4,384,256]{2,1,0:T(8,128)(2,1)}, bf16[4,384,256]{2,1,0:T(8,128)(2,1)}) custom-call(s32[3]{0:T(128)} %compare_select_fusion.5.place, bf16[384,256]{1,0:T(8,128)(2,1)} %bitcast.88, bf16[384,256]{1,0:T(8,128)(2,1)} %copy-done.14, bf16[384,256]{1,0:T(8,128)(2,1)} %copy-done.15, bf16[384,256]{1,0:T(8,128)(2,1)} %copy-done.16, ...), custom_call_target="tpu_custom_call" | custom-call | tf_op jit(solution)/shard_map/pallas_call | solution.py:45
  106.6 3.6 %collective-permute-start.16 = (bf16[384,256]{1,0:T(8,128)(2,1)S(1)}, bf16[384,256]{1,0:T(8,128)(2,1)S(1)}, u32[]{:S(2)}, u32[]{:S(2)}) collective-permute-start(bf16[384,256]{1,0:T(8,128)(2,1)S(1)} %get-tuple-element.51), channel_id=1, source_target_pairs={{0,8},{4,12},{8,0},{12,4},{1,9},{5,13},{9,1},{13,5},{2,10},{6,14},... | collective-permute-start | bytes 589832 | tf_op jit(solution)/shard_map/ppermute | solution.py:312
  118.3 3.1 %collective-permute-start.17 = (bf16[8,24,256]{2,1,0:T(8,128)(2,1)S(1)}, bf16[8,24,256]{2,1,0:T(8,128)(2,1)S(1)}, u32[]{:S(2)}, u32[]{:S(2)}) collective-permute-start(bf16[8,24,256]{2,1,0:T(8,128)(2,1)S(1)} %bitcast.92), channel_id=1, source_target_pairs={{0,1},{1,0},{2,3},{3,2},{4,5},{5,4},{6,7},{7,6},{8,9},{9,8},{10,11... | collective-permute-start | bytes 294920 | tf_op jit(solution)/shard_map/ppermute | solution.py:320
  121.4 3.1 %collective-permute-done.17 = bf16[8,24,256]{2,1,0:T(8,128)(2,1)S(1)} collective-permute-done((bf16[8,24,256]{2,1,0:T(8,128)(2,1)S(1)}, bf16[8,24,256]{2,1,0:T(8,128)(2,1)S(1)}, u32[]{:S(2)}, u32[]{:S(2)}) %collective-permute-start.17) | collective-permute-done | bytes 98336 | tf_op jit(solution)/shard_map/ppermute | solution.py:320
  125.1 14.5 %all_to_all.25 = bf16[16,24,256]{2,1,0:T(8,128)(2,1)S(1)} all-to-all(bf16[16,24,256]{2,1,0:T(8,128)(2,1)S(1)} %gather_fusion.4), channel_id=1, replica_groups=mesh['yl'=2,'z'=8,'x'=4,'core'=2,'yh'=2] {'yl','z'}, dimensions={0} | all-to-all | bytes 393216 | tf_op jit(solution)/shard_map/all_to_all | solution.py:331
  139.6 3.6 %collective-permute-start.18 = (bf16[384,256]{1,0:T(8,128)(2,1)S(1)}, bf16[384,256]{1,0:T(8,128)(2,1)S(1)}, u32[]{:S(2)}, u32[]{:S(2)}) collective-permute-start(bf16[384,256]{1,0:T(8,128)(2,1)S(1)} %bitcast.70), channel_id=1, source_target_pairs={{0,4},{4,8},{8,12},{12,0},{1,5},{5,9},{9,13},{13,1},{2,6},{6,10},{... | collective-permute-start | bytes 589832 | tf_op jit(solution)/shard_map/ppermute | solution.py:312
  147.5 2.9 %collective-permute-done.19.refs_2_ = bf16[384,256]{1,0:T(8,128)(2,1)S(1)} collective-permute-done((bf16[384,256]{1,0:T(8,128)(2,1)S(1)}, bf16[384,256]{1,0:T(8,128)(2,1)S(1)}, u32[]{:S(2)}, u32[]{:S(2)}) %collective-permute-start.19) | collective-permute-done | bytes 196640 | tf_op jit(solution)/shard_map/ppermute | solution.py:312
  160.4 7.4 %shard_map.187 = (bf16[8,64,384]{2,1,0:T(8,128)(2,1)S(1)}, bf16[8,64,384]{2,1,0:T(8,128)(2,1)S(1)}, bf16[8,64,384]{2,1,0:T(8,128)(2,1)S(1)}, bf16[8,64,384]{2,1,0:T(8,128)(2,1)S(1)}) custom-call(s32[3]{0:T(128)S(1)} %copy-done.12, bf16[4,384,64]{2,1,0:T(8,128)(2,1)S(1)} %get-tuple-element.34.refs_0_, bf16[2048,384]{1,0:T(8,128)(2,1)S(1)} %copy-done.2, ...), custom_call_target="tpu_custom_call" | custom-call | tf_op jit(solution)/shard_map/pallas_call | solution.py:45
  173.4 3.9 %all-to-all-start.4 = ((bf16[8,64,256]{2,1,0:T(8,128)(2,1)}), bf16[8,64,256]{2,1,0:T(8,128)(2,1)S(1)}, u32[]{:S(2)}, u32[]{:S(2)}) async-start(bf16[8,64,256]{2,1,0:T(8,128)(2,1)} %add_convert_fusion.1), calls=%async_computation.4 | async-start | bytes 524288 | tf_op jit(solution)/shard_map/all_to_all | solution.py:371
  177.3 11.2 %collective-permute-done.23 = bf16[8,64,384]{2,1,0:T(8,128)(2,1)} collective-permute-done((bf16[8,64,384]{2,1,0:T(8,128)(2,1)S(1)}, bf16[8,64,384]{2,1,0:T(8,128)(2,1)}, u32[]{:S(2)}, u32[]{:S(2)}) %collective-permute-start.23) | collective-permute-done | bytes 393248 | tf_op jit(solution)/shard_map/ppermute | solution.py:327
  190.7 3.5 %all-to-all-start.3 = ((bf16[8,64,384]{2,1,0:T(8,128)(2,1)}), bf16[8,64,384]{2,1,0:T(8,128)(2,1)S(1)}, u32[]{:S(2)}, u32[]{:S(2)}) async-start(bf16[8,64,384]{2,1,0:T(8,128)(2,1)} %add_convert_fusion), calls=%async_computation.3 | async-start | bytes 786432 | tf_op jit(solution)/shard_map/all_to_all | solution.py:371
  194.8 13.4 %all-to-all-done.3 = bf16[8,64,384]{2,1,0:T(8,128)(2,1)S(1)} async-done(((bf16[8,64,384]{2,1,0:T(8,128)(2,1)}), bf16[8,64,384]{2,1,0:T(8,128)(2,1)S(1)}, u32[]{:S(2)}, u32[]{:S(2)}) %all-to-all-start.3) | async-done | bytes 393248 | tf_op jit(solution)/shard_map/all_to_all | solution.py:371
  (128 shorter events, 64.1 us)
Async XLA Ops:
  16.5 7.9 %collective-permute-start.2 = (bf16[384,256]{1,0:T(8,128)(2,1)S(1)}, bf16[384,256]{1,0:T(8,128)(2,1)S(1)}, u32[]{:S(2)}, u32[]{:S(2)}) collective-permute-start(bf16[384,256]{1,0:T(8,128)(2,1)S(1)} %get-tuple-element.55), channel_id=1, source_target_pairs={{0,12},{4,0},{8,4},{12,8},{1,13},{5,1},{9,5},{13,9},{2,14},{6,2},{... | collective-permute-start | bytes 589832 | tf_op jit(solution)/shard_map/ppermute | solution.py:312
  17.3 9.6 %collective-permute-start.3 = (bf16[384,256]{1,0:T(8,128)(2,1)S(1)}, bf16[384,256]{1,0:T(8,128)(2,1)S(1)}, u32[]{:S(2)}, u32[]{:S(2)}) collective-permute-start(bf16[384,256]{1,0:T(8,128)(2,1)S(1)} %get-tuple-element.54), channel_id=1, source_target_pairs={{0,8},{4,12},{8,0},{12,4},{1,9},{5,13},{9,1},{13,5},{2,10},{6,14},... | collective-permute-start | bytes 589832 | tf_op jit(solution)/shard_map/ppermute | solution.py:312
  28.7 18.1 %all-to-all-start = ((bf16[16,24,256]{2,1,0:T(8,128)(2,1)}), bf16[16,24,256]{2,1,0:T(8,128)(2,1)S(1)}, u32[]{:S(2)}, u32[]{:S(2)}) async-start(bf16[16,24,256]{2,1,0:T(8,128)(2,1)} %bitcast.10), calls=%async_computation | async-start | bytes 393216 | tf_op jit(solution)/shard_map/all_to_all | solution.py:331
  46.8 23.2 %all-to-all-start.1 = ((bf16[16,24,1024]{2,1,0:T(8,128)(2,1)}), bf16[16,24,1024]{2,1,0:T(8,128)(2,1)S(1)}, u32[]{:S(2)}, u32[]{:S(2)}) async-start(bf16[16,24,1024]{2,1,0:T(8,128)(2,1)} %bitcast.17), calls=%async_computation.1 | async-start | bytes 1572864 | tf_op jit(solution)/shard_map/all_to_all | solution.py:331
  58.0 16.2 %collective-permute-start.5 = (bf16[384,256]{1,0:T(8,128)(2,1)S(1)}, bf16[384,256]{1,0:T(8,128)(2,1)S(1)}, u32[]{:S(2)}, u32[]{:S(2)}) collective-permute-start(bf16[384,256]{1,0:T(8,128)(2,1)S(1)} %bitcast.84), channel_id=1, source_target_pairs={{0,4},{4,8},{8,12},{12,0},{1,5},{5,9},{9,13},{13,1},{2,6},{6,10},{... | collective-permute-start | bytes 589832 | tf_op jit(solution)/shard_map/ppermute | solution.py:312
  62.0 12.3 %collective-permute-start.6 = (bf16[384,256]{1,0:T(8,128)(2,1)S(1)}, bf16[384,256]{1,0:T(8,128)(2,1)S(1)}, u32[]{:S(2)}, u32[]{:S(2)}) collective-permute-start(bf16[384,256]{1,0:T(8,128)(2,1)S(1)} %bitcast.85), channel_id=1, source_target_pairs={{0,8},{4,12},{8,0},{12,4},{1,9},{5,13},{9,1},{13,5},{2,10},{6,14},... | collective-permute-start | bytes 589832 | tf_op jit(solution)/shard_map/ppermute | solution.py:312
  63.2 11.1 %collective-permute-start.7 = (bf16[384,256]{1,0:T(8,128)(2,1)S(1)}, bf16[384,256]{1,0:T(8,128)(2,1)S(1)}, u32[]{:S(2)}, u32[]{:S(2)}) collective-permute-start(bf16[384,256]{1,0:T(8,128)(2,1)S(1)} %bitcast.86), channel_id=1, source_target_pairs={{0,12},{4,0},{8,4},{12,8},{1,13},{5,1},{9,5},{13,9},{2,14},{6,2},{... | collective-permute-start | bytes 589832 | tf_op jit(solution)/shard_map/ppermute | solution.py:312
  71.3 9.6 %collective-permute-start.10 = (bf16[8,24,1024]{2,1,0:T(8,128)(2,1)}, bf16[8,24,1024]{2,1,0:T(8,128)(2,1)}, u32[]{:S(2)}, u32[]{:S(2)}) collective-permute-start(bf16[8,24,1024]{2,1,0:T(8,128)(2,1)} %gather_fusion.3), channel_id=1, source_target_pairs={{0,1},{1,0},{2,3},{3,2},{4,5},{5,4},{6,7},{7,6},{8,9},{9,8},{10,11... | collective-permute-start | bytes 1179656 | tf_op jit(solution)/shard_map/ppermute | solution.py:320
  75.3 14.4 %collective-permute-start.9 = (bf16[3,384,256]{2,1,0:T(8,128)(2,1)}, bf16[3,384,256]{2,1,0:T(8,128)(2,1)}, u32[]{:S(2)}, u32[]{:S(2)}) collective-permute-start(bf16[3,384,256]{2,1,0:T(8,128)(2,1)} %pad_maximum_fusion), channel_id=1, source_target_pairs={{0,2},{2,0},{1,3},{3,1},{4,6},{6,4},{5,7},{7,5},{8,10},{10,8},{9,1... | collective-permute-start | bytes 1769480 | tf_op jit(solution)/shard_map/ppermute | solution.py:316
  80.9 8.7 %collective-permute-start.8 = (bf16[384,256]{1,0:T(8,128)(2,1)S(1)}, bf16[384,256]{1,0:T(8,128)(2,1)S(1)}, u32[]{:S(2)}, u32[]{:S(2)}) collective-permute-start(bf16[384,256]{1,0:T(8,128)(2,1)S(1)} %bitcast.87), channel_id=1, source_target_pairs={{0,2},{2,0},{1,3},{3,1},{4,6},{6,4},{5,7},{7,5},{8,10},{10,8},{9,1... | collective-permute-start | bytes 589832 | tf_op jit(solution)/shard_map/ppermute | solution.py:316
  104.2 7.7 %collective-permute-start.14 = (bf16[384,256]{1,0:T(8,128)(2,1)S(1)}, bf16[384,256]{1,0:T(8,128)(2,1)S(1)}, u32[]{:S(2)}, u32[]{:S(2)}) collective-permute-start(bf16[384,256]{1,0:T(8,128)(2,1)S(1)} %get-tuple-element.50), channel_id=1, source_target_pairs={{0,4},{4,8},{8,12},{12,0},{1,5},{5,9},{9,13},{13,1},{2,6},{6,10},{... | collective-permute-start | bytes 589832 | tf_op jit(solution)/shard_map/ppermute | solution.py:312
  106.5 7.8 %collective-permute-start.15 = (bf16[384,256]{1,0:T(8,128)(2,1)S(1)}, bf16[384,256]{1,0:T(8,128)(2,1)S(1)}, u32[]{:S(2)}, u32[]{:S(2)}) collective-permute-start(bf16[384,256]{1,0:T(8,128)(2,1)S(1)} %get-tuple-element.52), channel_id=1, source_target_pairs={{0,12},{4,0},{8,4},{12,8},{1,13},{5,1},{9,5},{13,9},{2,14},{6,2},{... | collective-permute-start | bytes 589832 | tf_op jit(solution)/shard_map/ppermute | solution.py:312
  106.6 10.5 %collective-permute-start.16 = (bf16[384,256]{1,0:T(8,128)(2,1)S(1)}, bf16[384,256]{1,0:T(8,128)(2,1)S(1)}, u32[]{:S(2)}, u32[]{:S(2)}) collective-permute-start(bf16[384,256]{1,0:T(8,128)(2,1)S(1)} %get-tuple-element.51), channel_id=1, source_target_pairs={{0,8},{4,12},{8,0},{12,4},{1,9},{5,13},{9,1},{13,5},{2,10},{6,14},... | collective-permute-start | bytes 589832 | tf_op jit(solution)/shard_map/ppermute | solution.py:312
  139.6 7.9 %collective-permute-start.18 = (bf16[384,256]{1,0:T(8,128)(2,1)S(1)}, bf16[384,256]{1,0:T(8,128)(2,1)S(1)}, u32[]{:S(2)}, u32[]{:S(2)}) collective-permute-start(bf16[384,256]{1,0:T(8,128)(2,1)S(1)} %bitcast.70), channel_id=1, source_target_pairs={{0,4},{4,8},{8,12},{12,0},{1,5},{5,9},{9,13},{13,1},{2,6},{6,10},{... | collective-permute-start | bytes 589832 | tf_op jit(solution)/shard_map/ppermute | solution.py:312
  143.3 7.2 %collective-permute-start.19 = (bf16[384,256]{1,0:T(8,128)(2,1)S(1)}, bf16[384,256]{1,0:T(8,128)(2,1)S(1)}, u32[]{:S(2)}, u32[]{:S(2)}) collective-permute-start(bf16[384,256]{1,0:T(8,128)(2,1)S(1)} %bitcast.71), channel_id=1, source_target_pairs={{0,8},{4,12},{8,0},{12,4},{1,9},{5,13},{9,1},{13,5},{2,10},{6,14},... | collective-permute-start | bytes 589832 | tf_op jit(solution)/shard_map/ppermute | solution.py:312
  143.3 7.2 %collective-permute-start.20 = (bf16[384,256]{1,0:T(8,128)(2,1)S(1)}, bf16[384,256]{1,0:T(8,128)(2,1)S(1)}, u32[]{:S(2)}, u32[]{:S(2)}) collective-permute-start(bf16[384,256]{1,0:T(8,128)(2,1)S(1)} %bitcast.72), channel_id=1, source_target_pairs={{0,12},{4,0},{8,4},{12,8},{1,13},{5,1},{9,5},{13,9},{2,14},{6,2},{... | collective-permute-start | bytes 589832 | tf_op jit(solution)/shard_map/ppermute | solution.py:312
  155.3 15.8 %collective-permute-start.26 = (bf16[8,64,256]{2,1,0:T(8,128)(2,1)S(1)}, bf16[8,64,256]{2,1,0:T(8,128)(2,1)S(1)}, u32[]{:S(2)}, u32[]{:S(2)}) collective-permute-start(bf16[8,64,256]{2,1,0:T(8,128)(2,1)S(1)} %get-tuple-element.45), channel_id=1, source_target_pairs={{0,128},{128,1},{1,129},{129,0},{2,130},{130,3},{3,131},{131,2},{4... | collective-permute-start | bytes 786440 | tf_op jit(solution)/shard_map/ppermute | solution.py:327
  156.4 16.2 %collective-permute-start.27 = (bf16[8,64,256]{2,1,0:T(8,128)(2,1)S(1)}, bf16[8,64,256]{2,1,0:T(8,128)(2,1)S(1)}, u32[]{:S(2)}, u32[]{:S(2)}) collective-permute-start(bf16[8,64,256]{2,1,0:T(8,128)(2,1)S(1)} %get-tuple-element.46), channel_id=1, source_target_pairs={{0,129},{128,0},{1,128},{129,1},{2,131},{130,2},{3,130},{131,3},{4... | collective-permute-start | bytes 786440 | tf_op jit(solution)/shard_map/ppermute | solution.py:327
  158.6 13.9 %collective-permute-start.28 = (bf16[8,64,256]{2,1,0:T(8,128)(2,1)S(1)}, bf16[8,64,256]{2,1,0:T(8,128)(2,1)S(1)}, u32[]{:S(2)}, u32[]{:S(2)}) collective-permute-start(bf16[8,64,256]{2,1,0:T(8,128)(2,1)S(1)} %get-tuple-element.47), channel_id=1, source_target_pairs={{0,1},{128,129},{1,0},{129,128},{2,3},{130,131},{3,2},{131,130},{4... | collective-permute-start | bytes 786440 | tf_op jit(solution)/shard_map/ppermute | solution.py:327
  167.8 20.7 %collective-permute-start.23 = (bf16[8,64,384]{2,1,0:T(8,128)(2,1)S(1)}, bf16[8,64,384]{2,1,0:T(8,128)(2,1)}, u32[]{:S(2)}, u32[]{:S(2)}) collective-permute-start(bf16[8,64,384]{2,1,0:T(8,128)(2,1)S(1)} %get-tuple-element.41), channel_id=1, source_target_pairs={{0,128},{128,1},{1,129},{129,0},{2,130},{130,3},{3,131},{131,2},{4... | collective-permute-start | bytes 1179656 | tf_op jit(solution)/shard_map/ppermute | solution.py:327
  168.3 20.2 %collective-permute-start.24 = (bf16[8,64,384]{2,1,0:T(8,128)(2,1)S(1)}, bf16[8,64,384]{2,1,0:T(8,128)(2,1)}, u32[]{:S(2)}, u32[]{:S(2)}) collective-permute-start(bf16[8,64,384]{2,1,0:T(8,128)(2,1)S(1)} %get-tuple-element.42), channel_id=1, source_target_pairs={{0,129},{128,0},{1,128},{129,1},{2,131},{130,2},{3,130},{131,3},{4... | collective-permute-start | bytes 1179656 | tf_op jit(solution)/shard_map/ppermute | solution.py:327
  171.1 17.3 %collective-permute-start.25 = (bf16[8,64,384]{2,1,0:T(8,128)(2,1)S(1)}, bf16[8,64,384]{2,1,0:T(8,128)(2,1)}, u32[]{:S(2)}, u32[]{:S(2)}) collective-permute-start(bf16[8,64,384]{2,1,0:T(8,128)(2,1)S(1)} %get-tuple-element.43), channel_id=1, source_target_pairs={{0,1},{128,129},{1,0},{129,128},{2,3},{130,131},{3,2},{131,130},{4... | collective-permute-start | bytes 1179656 | tf_op jit(solution)/shard_map/ppermute | solution.py:327
  173.4 17.2 %all-to-all-start.4 = ((bf16[8,64,256]{2,1,0:T(8,128)(2,1)}), bf16[8,64,256]{2,1,0:T(8,128)(2,1)S(1)}, u32[]{:S(2)}, u32[]{:S(2)}) async-start(bf16[8,64,256]{2,1,0:T(8,128)(2,1)} %add_convert_fusion.1), calls=%async_computation.4 | async-start | bytes 524288 | tf_op jit(solution)/shard_map/all_to_all | solution.py:371
  190.7 17.5 %all-to-all-start.3 = ((bf16[8,64,384]{2,1,0:T(8,128)(2,1)}), bf16[8,64,384]{2,1,0:T(8,128)(2,1)S(1)}, u32[]{:S(2)}, u32[]{:S(2)}) async-start(bf16[8,64,384]{2,1,0:T(8,128)(2,1)} %add_convert_fusion), calls=%async_computation.3 | async-start | bytes 786432 | tf_op jit(solution)/shard_map/all_to_all | solution.py:371
  (33 other events, 399.5 us)
